TPU v7x, 768 devices: a whole 4x8x12 slice. The times are simulated.
768 devices in a mesh: dp: 64 (over x, y, core), fsdp: 12 (over z).
Axes of the slice: x: 4, y: 8, z: 12, core: 2. Of those that a mesh axis runs over, the one named last changes fastest.
Arguments:
- grads: float32 [768, 2304, 128], P(('dp', 'fsdp')), may hold values from -2.5 to 2.5
- last_peak: float32 [2304], replicated, may hold values from 0.05 to 0.8
- master: float32 [2304, 128], P(('dp', 'fsdp')), may hold values from -6 to 6
- moment1: float32 [2304, 128], P(('dp', 'fsdp')), may hold values from -6 to 6
- moment2: float32 [2304, 128], P(('dp', 'fsdp')), may hold values from 0.25 to 8
Outputs:
- new_master: float32 [2304, 128], P(('dp', 'fsdp'))
- new_moment1: float32 [2304, 128], P(('dp', 'fsdp'))
- new_moment2: float32 [2304, 128], P(('dp', 'fsdp'))
- weights: bfloat16 [2304, 128], replicated
- block_peak: float32 [2304], replicated
All inputs are finite; a program needn't handle non-finite values.
Results may differ from a plain program's by a relative error of at most 0.0035.
Values may be sent and summed in bfloat16 or wider, within the bound.
A program may use at most 64 MiB of HBM per device.

v0:
```python
import functools

import jax
import jax.numpy as jnp
from jax import lax
from jax.sharding import Mesh
from jax.sharding import PartitionSpec as P

STEP_COUNT = 10
DP_FSDP = ("dp_0", "dp_1", "dp_2", "fsdp")
DP = ("dp_0", "dp_1", "dp_2")


code_limit = 448.0
peak_floor = 0.05
beta_one = 0.9
beta_two = 0.95
learn_rate = 0.05
decay_rate = 0.1
epsilon = 1e-08


def over_axes(value, axes):
    return functools.reduce(lax.pmax, axes, value)


def cut_along(value, dim, peers):
    before, after = (value.shape[:dim], value.shape[dim + 1 :])
    return jnp.moveaxis(value.reshape(*before, peers, -1, *after), dim, 0)


def summed_on_arrival(value, axis, dim):
    pieces = cut_along(value, dim, lax.axis_size(axis))
    arrived = lax.all_to_all(pieces, axis, split_axis=0, concat_axis=0, tiled=True)
    return arrived.astype(jnp.float32).sum(axis=0)


def summed_on_arrival_2(value, axis, dim):
    peers = lax.axis_size(axis)
    pieces = lax.all_to_all(cut_along(value, dim, peers), axis, 0, 0, tiled=True)
    return jnp.sum(pieces, axis=0)


def from_everyone(value, axis):
    copies = jnp.broadcast_to(value, (lax.axis_size(axis), *value.shape))
    return lax.all_to_all(copies, axis, split_axis=0, concat_axis=0, tiled=True)


def joined_along(pieces, dim):
    dims = list(pieces.shape[1:])
    dims[dim] *= pieces.shape[0]
    return jnp.moveaxis(pieces, 0, dim).reshape(dims)


def gathered_copies(value, axis, dim):
    pieces = from_everyone(value, axis)
    return joined_along(pieces, dim)


def quantize(rows, inverse):
    codes = jnp.clip(rows * inverse[:, None], -code_limit, code_limit).astype(jnp.bfloat16)
    return lax.optimization_barrier(codes).astype(jnp.float32)


def adamw(gradient, master, moment1, moment2):
    first = beta_one * moment1 + (1.0 - beta_one) * gradient
    second = beta_two * moment2 + (1.0 - beta_two) * gradient * gradient
    corrected_one = first / (1.0 - beta_one**STEP_COUNT)
    corrected_two = second / (1.0 - beta_two**STEP_COUNT)
    updated = master - learn_rate * (
        corrected_one / (jnp.sqrt(corrected_two) + epsilon) + decay_rate * master
    )
    return (updated, first, second)


def body(grads, last_peak, master, moment1, moment2):
    local = grads[0]
    peak = over_axes(jnp.max(jnp.abs(local), axis=1), DP_FSDP)
    floored = jnp.maximum(last_peak, peak_floor)
    inverse = code_limit / floored
    scale = floored / code_limit
    owned = master.shape[0]
    width = master.shape[1]
    first_row = lax.axis_index(DP_FSDP) * owned
    outer_count = lax.axis_size(DP)
    inner_count = lax.axis_size("fsdp")
    terms = quantize(local, inverse).reshape(outer_count, inner_count, owned, width)
    grouped = summed_on_arrival(terms.astype(jnp.bfloat16), "fsdp", 1)
    summed = summed_on_arrival_2(grouped, DP, 0).reshape(owned, width)
    own_scale = lax.dynamic_slice_in_dim(scale, first_row, owned, 0)
    gradient = summed * own_scale[:, None]
    updated, first, second = adamw(gradient, master, moment1, moment2)
    rounded = updated.astype(jnp.bfloat16)
    grouped_rows = gathered_copies(rounded, "fsdp", 0)
    weights = gathered_copies(grouped_rows, DP, 0)
    return (updated, first, second, weights, peak)


def solution(mesh):
    torus = Mesh(
        mesh.devices.reshape(4, 8, 2, mesh.shape["fsdp"]), ("dp_0", "dp_1", "dp_2", "fsdp")
    )
    in_specs = (P(DP_FSDP, None, None), P(), P(DP_FSDP, None), P(DP_FSDP, None), P(DP_FSDP, None))
    out_specs = (P(DP_FSDP, None), P(DP_FSDP, None), P(DP_FSDP, None), P(), P())
    return jax.shard_map(body, mesh=torus, in_specs=in_specs, out_specs=out_specs, check_vma=False)
```

profile of v0, /device:TPU:8, one launch (start us, length us, event | category | flops | bytes accessed | tf_op | source)
XLA Modules:
  0.0 177.1 jit_solution(17161139886809503425)
XLA Ops:
  0.6 0.7 broadcast_maximum_fusion
  1.3 2.0 %fusion.2 = (f32[2304]{0:T(1024)S(1)}, bf16[2304,128]{1,0:T(8,128)(2,1)S(1)}) fusion(f32[1,2304,128]{2,1,0:T(8,128)} %param.5, f32[2304]{0:T(1024)S(1)} %get-tuple-element.12), kind=kLoop, calls=%fused_computation.4 | loop fusion | flops 1472256 | bytes 1787904 | tf_op jit(solution)/shard_map/reduce_max | solution.py:78
  3.3 0.3 convert_element_type.22
  3.6 0.2 copy.11
  3.8 0.0 copy-start
  3.8 0.0 copy-start.1
  3.9 0.0 copy-start.2
  3.9 42.0 %all_to_all.20 = bf16[12,64,1,3,128]{4,1,3,2,0:T(8,128)(2,1)S(1)} all-to-all(bf16[12,64,1,3,128]{4,1,3,2,0:T(8,128)(2,1)S(1)} %copy.11), channel_id=1, replica_groups=mesh['dp_0'=4,'dp_1'=8,'dp_2'=2,'fsdp'=12] {'fsdp'}, dimensions={0} | all-to-all | bytes 1179648 | tf_op jit(solution)/shard_map/all_to_all | solution.py:34
  45.8 0.1 convert_reduce_fusion
  45.9 0.7 copy.12
  46.7 10.6 %all-to-all-start.1 = ((f32[64,1,1,3,128]{4,2,3,1,0:T(1,128)}), f32[64,1,1,3,128]{4,2,3,1,0:T(1,128)S(1)}, u32[]{:S(2)}, u32[]{:S(2)}) async-start(f32[64,1,1,3,128]{4,2,3,1,0:T(1,128)} %copy.12), calls=%async_computation.1 | async-start | bytes 196608 | tf_op jit(solution)/shard_map/all_to_all | solution.py:40
  57.3 0.1 dynamic-slice_multiply_fusion
  57.4 9.4 %all-to-all-done.1 = f32[64,1,1,3,128]{4,2,3,1,0:T(1,128)S(1)} async-done(((f32[64,1,1,3,128]{4,2,3,1,0:T(1,128)}), f32[64,1,1,3,128]{4,2,3,1,0:T(1,128)S(1)}, u32[]{:S(2)}, u32[]{:S(2)}) %all-to-all-start.1) | async-done | bytes 98336 | tf_op jit(solution)/shard_map/all_to_all | solution.py:40
  66.7 0.1 reduce_sum.19
  66.8 0.0 copy-done
  66.8 0.0 copy-done.1
  66.8 0.0 copy-done.2
  66.9 0.7 fusion.4
  67.5 12.9 %all_to_all.21 = bf16[12,3,128]{2,1,0:T(4,128)(2,1)S(1)} all-to-all(bf16[12,3,128]{2,1,0:T(4,128)(2,1)S(1)} %broadcast_in_dim.8), channel_id=1, replica_groups=mesh['dp_0'=4,'dp_1'=8,'dp_2'=2,'fsdp'=12] {'fsdp'}, dimensions={0} | all-to-all | bytes 18432 | tf_op jit(solution)/shard_map/all_to_all | solution.py:46
  80.5 0.9 broadcast_in_dim.9
  81.4 5.2 %all-to-all-start.3 = ((bf16[64,36,128]{2,1,0:T(8,128)(2,1)}), bf16[64,36,128]{2,1,0:T(8,128)(2,1)S(1)}, u32[]{:S(2)}, u32[]{:S(2)}) async-start(bf16[64,36,128]{2,1,0:T(8,128)(2,1)} %broadcast_in_dim.9), calls=%async_computation.3 | async-start | bytes 1310720 | tf_op jit(solution)/shard_map/all_to_all | solution.py:46
  86.5 17.3 %pmax.28 = f32[2304]{0:T(1024)S(1)} all-reduce(f32[2304]{0:T(1024)S(1)} %get-tuple-element.9), channel_id=1, replica_groups=mesh['dp_0'=4,'dp_1'=8,'dp_2'=2,'fsdp'=12] {'dp_0'}, use_global_device_ids=true, to_apply=%region_3.0 | all-reduce | flops 2304 | bytes 18432 | tf_op jit(solution)/shard_map/pmax | solution.py:24
  103.8 28.2 %pmax.29 = f32[2304]{0:T(1024)S(1)} all-reduce(f32[2304]{0:T(1024)S(1)} %pmax.28), channel_id=1, replica_groups=mesh['dp_0'=4,'dp_1'=8,'dp_2'=2,'fsdp'=12] {'dp_1'}, use_global_device_ids=true, to_apply=%region_4.0 | all-reduce | flops 2304 | bytes 18432 | tf_op jit(solution)/shard_map/pmax | solution.py:24
  132.1 3.3 %pmax.30 = f32[2304]{0:T(1024)S(1)} all-reduce(f32[2304]{0:T(1024)S(1)} %pmax.29), channel_id=1, replica_groups=mesh['dp_0'=4,'dp_1'=8,'dp_2'=2,'fsdp'=12] {'dp_2'}, use_global_device_ids=true, to_apply=%region_5.6 | all-reduce | flops 2304 | bytes 18432 | tf_op jit(solution)/shard_map/pmax | solution.py:24
  135.3 40.9 %pmax.31 = f32[2304]{0:T(1024)} all-reduce(f32[2304]{0:T(1024)S(1)} %pmax.30), channel_id=1, replica_groups=mesh['dp_0'=4,'dp_1'=8,'dp_2'=2,'fsdp'=12] {'fsdp'}, use_global_device_ids=true, to_apply=%region_6.7 | all-reduce | flops 2304 | bytes 18432 | tf_op jit(solution)/shard_map/pmax | solution.py:24
  176.2 0.0 all-to-all-done.3
  176.2 0.9 reshape.41
  (2 shorter events, 0.0 us)
Async XLA Ops:
  3.8 63.0 %copy-start = (f32[3,128]{1,0:T(4,128)S(1)}, f32[3,128]{1,0:T(4,128)}, u32[]{:S(2)}) copy-start(f32[3,128]{1,0:T(4,128)} %param.7) | copy-start | bytes 4612
  3.8 63.0 %copy-start.1 = (f32[3,128]{1,0:T(4,128)S(1)}, f32[3,128]{1,0:T(4,128)}, u32[]{:S(2)}) copy-start(f32[3,128]{1,0:T(4,128)} %param.8) | copy-start | bytes 4612
  3.9 63.0 %copy-start.2 = (f32[3,128]{1,0:T(4,128)S(1)}, f32[3,128]{1,0:T(4,128)}, u32[]{:S(2)}) copy-start(f32[3,128]{1,0:T(4,128)} %param.9) | copy-start | bytes 4612
  46.7 20.1 %all-to-all-start.1 = ((f32[64,1,1,3,128]{4,2,3,1,0:T(1,128)}), f32[64,1,1,3,128]{4,2,3,1,0:T(1,128)S(1)}, u32[]{:S(2)}, u32[]{:S(2)}) async-start(f32[64,1,1,3,128]{4,2,3,1,0:T(1,128)} %copy.12), calls=%async_computation.1 | async-start | bytes 196608 | tf_op jit(solution)/shard_map/all_to_all | solution.py:40
  81.4 94.8 %all-to-all-start.3 = ((bf16[64,36,128]{2,1,0:T(8,128)(2,1)}), bf16[64,36,128]{2,1,0:T(8,128)(2,1)S(1)}, u32[]{:S(2)}, u32[]{:S(2)}) async-start(bf16[64,36,128]{2,1,0:T(8,128)(2,1)} %broadcast_in_dim.9), calls=%async_computation.3 | async-start | bytes 1310720 | tf_op jit(solution)/shard_map/all_to_all | solution.py:46
where the time goes:
time: 178 us; the launch traced here: 177 us
  blocking collectives  145 us (81%)
  starting transfers between devices  15.7 us (9%)
  waiting for transfers between devices  9.38 us (5%)
  other arithmetic  3.63 us (2%)
  local copies, waits for them, and re-layouts  3.13 us (2%)
    pmax x4, blocking collectives, over_axes(): return functools.reduce(lax.pmax, axes, value)  89.7 us
    all_to_all x1, blocking collectives, summed_on_arrival(): lax.all_to_all(pieces, axis, split_axis=0, concat_axis=0, tiled=True)  42 us
    all_to_all x1, blocking collectives, from_everyone(): return lax.all_to_all(copies, axis, split_axis=0, concat_axis=0, tiled=True)  12.9 us
    all_to_all x1, starting transfers between devices, summed_on_arrival_2(): lax.all_to_all(cut_along(value, dim, peers), axis, 0, 0, tiled=True)  10.6 us
    all_to_all x1, waiting for transfers between devices, summed_on_arrival_2(): lax.all_to_all(cut_along(value, dim, peers), axis, 0, 0, tiled=True)  9.37 us
    all_to_all x1, starting transfers between devices, from_everyone(): return lax.all_to_all(copies, axis, split_axis=0, concat_axis=0, tiled=True)  5.16 us
  transfers between devices with their start and end apart: 2, of which 1 were waited for; matrix products, arithmetic and copies ran while one was open for 0% of the time, Pallas kernels for 0%

commit v1 on v0

v1 whole, which is shorter than its diff:
```python
import functools

import jax
import jax.numpy as jnp
from jax import lax
from jax.experimental import pallas as pl
from jax.experimental.pallas import tpu as pltpu
from jax.sharding import Mesh
from jax.sharding import PartitionSpec as P

STEP_COUNT = 10
AXES = ("dp_0", "dp_1", "dp_2", "fsdp")
MESH = pl.DeviceIdType.MESH

code_limit = 448.0
peak_floor = 0.05
beta_one = 0.9
beta_two = 0.95
learn_rate = 0.05
decay_rate = 0.1
epsilon = 1e-08

X, Y, C, Z = 4, 8, 2, 12
ROWS, WIDTH = 2304, 128
PIECE = ROWS // (X * C)
GROUP = ROWS // (X * Y)
SHARE = GROUP // C
OWNED = SHARE // Z
LANE_ROWS = ROWS // WIDTH
CHUNKS = 9


def adamw(gradient, master, moment1, moment2):
    first = beta_one * moment1 + (1.0 - beta_one) * gradient
    second = beta_two * moment2 + (1.0 - beta_two) * gradient * gradient
    corrected_one = first / (1.0 - beta_one**STEP_COUNT)
    corrected_two = second / (1.0 - beta_two**STEP_COUNT)
    updated = master - learn_rate * (
        corrected_one / (jnp.sqrt(corrected_two) + epsilon) + decay_rate * master
    )
    return (updated, first, second)


def kernel(
    grads, last_peak, master, moment1, moment2,
    out_master, out_first, out_second, weights, out_peak,
    g, lp, state, stepped, codes, r1, pk1, rp1, t1, s1, p1, r2, rp2, s2, r3, p3, rp3,
    w3, gz, a36, ay, gy, rp4, t288, wb, pg, rp5, peak_lanes,
    load_sem, small_sem, out_sem,
    ss1, rs1, sp1, rps1, ss2, rs2, sp2, rps2, ss3, rs3, sp3, rps3,
    sz, rz, sy, ry, sp4, rps4, sx, rx, sp5, rps5, sd, rd, so,
):
    x, y, c, z = (lax.axis_index(a) for a in AXES)
    mine = 2 * x + c
    half = y // 4
    inside = lax.rem(y, 4)

    def at(xx=None, yy=None, cc=None, zz=None):
        where = {"dp_0": xx, "dp_1": yy, "dp_2": cc, "fsdp": zz}
        return {k: v for k, v in where.items() if v is not None}

    def remote(src, dst, send, recv, where):
        return pltpu.make_async_remote_copy(
            src_ref=src, dst_ref=dst, send_sem=send, recv_sem=recv, device_id=where, device_id_type=MESH
        )

    barrier = pltpu.get_barrier_semaphore()
    for d in range(1, Z):
        pl.semaphore_signal(barrier, inc=1, device_id=at(zz=lax.rem(z + d, Z)), device_id_type=MESH)
    for d in range(1, Y):
        for cc in range(C):
            pl.semaphore_signal(barrier, inc=1, device_id=at(yy=lax.rem(y + d, Y), cc=cc), device_id_type=MESH)
    for d in range(1, X):
        for cc in range(C):
            pl.semaphore_signal(barrier, inc=1, device_id=at(xx=lax.rem(x + d, X), cc=cc), device_id_type=MESH)
    pl.semaphore_signal(barrier, inc=1, device_id=at(cc=1 - c), device_id_type=MESH)

    step_rows = ROWS // CHUNKS
    lp_copy = pltpu.make_async_copy(last_peak, lp, small_sem.at[0])
    lp_copy.start()
    loads = [
        pltpu.make_async_copy(
            grads.at[pl.ds(i * step_rows, step_rows)], g.at[pl.ds(i * step_rows, step_rows)], load_sem.at[i]
        )
        for i in range(CHUNKS)
    ]
    for copy in loads:
        copy.start()
    state_copies = [
        pltpu.make_async_copy(src, state.at[i], small_sem.at[1 + i])
        for i, src in enumerate((master, moment1, moment2))
    ]
    for copy in state_copies:
        copy.start()
    lp_copy.wait()

    square = (WIDTH, WIDTH)
    row_at = lax.broadcasted_iota(jnp.int32, square, 0)
    lane_at = lax.broadcasted_iota(jnp.int32, square, 1)
    for i in range(CHUNKS):
        loads[i].wait()
        for j in range(step_rows // WIDTH):
            r = i * (step_rows // WIDTH) + j
            rows = pl.ds(r * WIDTH, WIDTH)
            inverse = code_limit / jnp.maximum(lp[pl.ds(r, 1), :], peak_floor)
            spread = jnp.where(row_at == lane_at, jnp.broadcast_to(inverse, square), 0.0)
            column = jnp.sum(spread, axis=1, keepdims=True)
            scaled = g[rows, :] * column
            codes[rows, :] = jnp.clip(scaled, -code_limit, code_limit).astype(jnp.bfloat16)

    tall = (GROUP, WIDTH)
    tall_row = lax.broadcasted_iota(jnp.int32, tall, 0)
    tall_lane = lax.broadcasted_iota(jnp.int32, tall, 1)

    for k in range(X * C):
        for i in range(4):
            rows = pl.ds((4 * k + i) * GROUP, GROUP)
            top = jnp.max(jnp.abs(g[rows, :]), axis=1, keepdims=True)
            laid = jnp.where(tall_row == tall_lane, jnp.broadcast_to(top, tall), 0.0)
            pk1[k, i : i + 1, :] = jnp.max(laid, axis=0, keepdims=True)

    first_row = (((x * Y + y) * C + c) * Z + z) * OWNED
    flat = lax.broadcasted_iota(jnp.int32, (LANE_ROWS, WIDTH), 0) * WIDTH + lax.broadcasted_iota(
        jnp.int32, (LANE_ROWS, WIDTH), 1
    )
    own_row = lax.broadcasted_iota(jnp.int32, (OWNED, WIDTH), 0)
    all_scales = jnp.maximum(lp[...], peak_floor) / code_limit
    scale = jnp.zeros((OWNED, WIDTH), jnp.float32)
    for j in range(OWNED):
        one = jnp.sum(jnp.where(flat == first_row + j, all_scales, 0.0), axis=(0, 1), keepdims=True)
        scale = jnp.where(own_row == j, jnp.broadcast_to(one, scale.shape), scale)

    pl.semaphore_wait(barrier, (Z - 1) + (Y - 1) * C + (X - 1) * C + 1)

    def code_rows(k):
        return codes.at[pl.ds(pl.multiple_of(k * PIECE, 16), PIECE)]

    sent1 = []
    for d in (4, 5, 3, 6, 2, 7, 1):
        k = lax.rem(mine + d, X * C)
        where = at(xx=k // 2, cc=lax.rem(k, 2))
        sent1.append(remote(code_rows(k), r1.at[mine], ss1.at[d], rs1.at[mine], where))
        sent1.append(remote(pk1.at[k], rp1.at[mine], sp1.at[d], rps1.at[mine], where))
    for copy in sent1:
        copy.start()
    for d in range(1, X * C):
        k = lax.rem(mine + d, X * C)
        remote(r1.at[k], r1.at[k], ss1.at[d], rs1.at[k], at(cc=1 - c)).wait_recv()

    block = 48
    for b in range(PIECE // block):
        own = codes[pl.ds(pl.multiple_of(mine * PIECE + b * block, 16), block), :]
        total = own.astype(jnp.float32)
        for d in range(1, X * C):
            k = lax.rem(mine + d, X * C)
            total = total + r1[k, pl.ds(b * block, block), :].astype(jnp.float32)
        t1[pl.ds(b * block, block), :] = total
    for m in range(8):
        s1[m] = t1[pl.ds(m * SHARE, SHARE), :]

    def to_y(d, cc):
        yy = 4 * c + lax.rem(inside + d, 4)
        m = 2 * lax.rem(inside + d, 4) + cc
        return remote(s1.at[m], r2.at[y], ss2.at[2 * d + cc], rs2.at[y], at(yy=yy, cc=cc))

    def peak_to_y(d, cc):
        yy = 4 * c + lax.rem(inside + d, 4)
        return remote(
            p1.at[lax.rem(inside + d, 4)], rp2.at[y], sp2.at[2 * d + cc], rps2.at[y], at(yy=yy, cc=cc)
        )

    for d in (2, 3, 1):
        for cc in range(C):
            to_y(d, cc).start()
    other = 1 - c

    def own_y(make, sems):
        yy = 4 * c + inside
        return make, sems, yy

    def to_y0(cc, index):
        yy = 4 * c + inside
        return remote(s1.at[2 * inside + cc], r2.at[y], ss2.at[index], rs2.at[y], at(yy=yy, cc=cc))

    def peak_to_y0(cc, index):
        yy = 4 * c + inside
        return remote(p1.at[inside], rp2.at[y], sp2.at[index], rps2.at[y], at(yy=yy, cc=cc))

    to_y0(other, 0).start()

    @pl.when(half != c)
    def _():
        to_y0(c, 1).start()

    @pl.when(half == c)
    def _():
        r2[y] = s1[2 * inside + c]

    for d in range(1, X * C):
        k = lax.rem(mine + d, X * C)
        remote(rp1.at[k], rp1.at[k], sp1.at[d], rps1.at[k], at(cc=1 - c)).wait_recv()
    top = pk1[mine]
    for d in range(1, X * C):
        top = jnp.maximum(top, rp1[lax.rem(mine + d, X * C)])
    for i in range(4):
        p1[i] = top[i : i + 1, :]
    for d in (2, 3, 1):
        for cc in range(C):
            peak_to_y(d, cc).start()
    peak_to_y0(other, 0).start()

    @pl.when(half != c)
    def _():
        peak_to_y0(c, 1).start()

    @pl.when(half == c)
    def _():
        rp2[y] = p1[inside]

    for d in range(1, Y):
        yy = lax.rem(y + d, Y)
        remote(r2.at[yy], r2.at[yy], ss2.at[0], rs2.at[yy], at(cc=1 - c)).wait_recv()

    @pl.when(half != c)
    def _():
        remote(r2.at[y], r2.at[y], ss2.at[0], rs2.at[y], at(cc=1 - c)).wait_recv()

    total = r2[0]
    for i in range(1, Y):
        total = total + r2[i]
    for i in range(Z):
        s2[i] = total[i * OWNED : (i + 1) * OWNED, :]

    def to_z(d):
        zz = lax.rem(z + d, Z)
        return remote(s2.at[zz], r3.at[z], ss3.at[d], rs3.at[z], at(zz=zz))

    far_z = (6, 7, 5, 8, 4, 9, 3, 10, 2, 11, 1)
    for d in far_z:
        to_z(d).start()

    for d in range(1, Y):
        yy = lax.rem(y + d, Y)
        remote(rp2.at[yy], rp2.at[yy], sp2.at[0], rps2.at[yy], at(cc=1 - c)).wait_recv()

    @pl.when(half != c)
    def _():
        remote(rp2.at[y], rp2.at[y], sp2.at[0], rps2.at[y], at(cc=1 - c)).wait_recv()

    top = rp2[0]
    for i in range(1, Y):
        top = jnp.maximum(top, rp2[i])
    p3[...] = top

    def peak_to_z(d):
        return remote(p3, rp3.at[z], sp3.at[d], rps3.at[z], at(zz=lax.rem(z + d, Z)))

    for d in far_z:
        peak_to_z(d).start()

    for copy in state_copies:
        copy.wait()
    for d in range(1, Z):
        zz = lax.rem(z + d, Z)
        remote(r3.at[zz], r3.at[zz], ss3.at[d], rs3.at[zz], at(zz=zz)).wait_recv()
    total = s2[z]
    for d in range(1, Z):
        total = total + r3[lax.rem(z + d, Z)]
    gradient = total * scale
    updated, first, second = adamw(gradient, state[0], state[1], state[2])
    w3[...] = updated.astype(jnp.bfloat16).astype(jnp.float32)
    stepped[0] = updated
    stepped[1] = first
    stepped[2] = second

    def give_z(d):
        return remote(w3, gz.at[z], sz.at[d], rz.at[z], at(zz=lax.rem(z + d, Z)))

    for d in far_z:
        give_z(d).start()
    gz[z] = w3[...]
    step_outs = [
        pltpu.make_async_copy(stepped.at[i], dst, out_sem.at[i])
        for i, dst in enumerate((out_master, out_first, out_second))
    ]
    for copy in step_outs:
        copy.start()

    for d in range(1, Z):
        zz = lax.rem(z + d, Z)
        remote(rp3.at[zz], rp3.at[zz], sp3.at[d], rps3.at[zz], at(zz=zz)).wait_recv()
    top = p3[...]
    for d in range(1, Z):
        top = jnp.maximum(top, rp3[lax.rem(z + d, Z)])
    rp4[y] = top

    def peak_give_y(d):
        return remote(rp4.at[y], rp4.at[y], sp4.at[d], rps4.at[y], at(yy=lax.rem(y + d, Y)))

    far_y = (4, 5, 3, 6, 2, 7, 1)
    for d in far_y:
        peak_give_y(d).start()

    for d in range(1, Z):
        zz = lax.rem(z + d, Z)
        remote(gz.at[zz], gz.at[zz], sz.at[d], rz.at[zz], at(zz=zz)).wait_recv()
    for i in range(Z):
        a36[pl.ds(i * OWNED, OWNED), :] = gz[i]
    ay[...] = a36[...].astype(jnp.bfloat16)

    slot = 2 * inside + c

    def give_y(d):
        return remote(ay, gy.at[slot], sy.at[d], ry.at[slot], at(yy=lax.rem(y + d, Y), cc=half))

    for d in far_y:
        give_y(d).start()

    @pl.when(half != c)
    def _():
        remote(ay, gy.at[slot], sy.at[0], ry.at[slot], at(cc=half)).start()

    @pl.when(half == c)
    def _():
        gy[slot] = ay[...]

    for d in range(1, Y):
        yy = lax.rem(y + d, Y)
        remote(rp4.at[yy], rp4.at[yy], sp4.at[d], rps4.at[yy], at(yy=yy)).wait_recv()
    for i in range(Y):
        pg[i : i + 1, :] = rp4[i]

    def peak_give_x(d):
        return remote(pg, rp5.at[x], sp5.at[d], rps5.at[x], at(xx=lax.rem(x + d, X)))

    for d in (2, 3, 1):
        peak_give_x(d).start()
    rp5[x] = pg[...]

    for m in range(8):
        @pl.when((half != c) | (m != slot))
        def _():
            remote(gy.at[m], gy.at[m], sy.at[0], ry.at[m], at(cc=1 - c)).wait_recv()

    for m in range(8):
        t288[pl.ds(m * SHARE, SHARE), :] = gy[m].astype(jnp.float32)
    wb[mine] = t288[...].astype(jnp.bfloat16)

    def out_rows(k):
        return weights.at[pl.ds(pl.multiple_of(k * PIECE, 16), PIECE)]

    def give_x(d):
        return remote(wb.at[mine], wb.at[mine], sx.at[d], rx.at[mine], at(xx=lax.rem(x + d, X)))

    def give_core(d):
        k = 2 * lax.rem(x + d, X) + c
        return remote(wb.at[k], out_rows(k), sd.at[d], rd.at[d], at(cc=1 - c))

    def keep(d):
        k = 2 * lax.rem(x + d, X) + c
        return pltpu.make_async_copy(wb.at[k], out_rows(k), so.at[d])

    for d in (2, 3, 1):
        give_x(d).start()
    give_core(0).start()
    keep(0).start()

    for d in range(1, X):
        xx = lax.rem(x + d, X)
        remote(rp5.at[xx], rp5.at[xx], sp5.at[d], rps5.at[xx], at(xx=xx)).wait_recv()
    lane_of = lax.broadcasted_iota(jnp.int32, (1, WIDTH), 1)
    for j in range(LANE_ROWS):
        line = jnp.zeros((1, WIDTH), jnp.float32)
        for n in range(X * Y):
            lo = GROUP * n - WIDTH * j
            if lo >= WIDTH or lo + GROUP <= 0:
                continue
            row = rp5[n // Y, n % Y : n % Y + 1, :]
            if lo % WIDTH:
                row = pltpu.roll(row, lo % WIDTH, 1)
            line = jnp.where((lane_of >= lo) & (lane_of < lo + GROUP), row, line)
        peak_lanes[j : j + 1, :] = line
    peak_out = pltpu.make_async_copy(peak_lanes, out_peak, out_sem.at[3])
    peak_out.start()

    for d in (1, 3, 2):
        xx = lax.rem(x + d, X)
        k = 2 * xx + c
        remote(wb.at[k], wb.at[k], sx.at[d], rx.at[k], at(xx=xx)).wait_recv()
        give_core(d).start()
        keep(d).start()

    for copy in sent1:
        copy.wait_send()
    for d in (2, 3, 1):
        for cc in range(C):
            to_y(d, cc).wait_send()
            peak_to_y(d, cc).wait_send()
    to_y0(other, 0).wait_send()
    peak_to_y0(other, 0).wait_send()

    @pl.when(half != c)
    def _():
        to_y0(c, 1).wait_send()
        peak_to_y0(c, 1).wait_send()
        remote(ay, gy.at[slot], sy.at[0], ry.at[slot], at(cc=half)).wait_send()

    for d in far_z:
        to_z(d).wait_send()
        peak_to_z(d).wait_send()
        give_z(d).wait_send()
    for d in far_y:
        peak_give_y(d).wait_send()
        give_y(d).wait_send()
    for d in (1, 2, 3):
        peak_give_x(d).wait_send()
        give_x(d).wait_send()
    for copy in step_outs:
        copy.wait()
    peak_out.wait()
    for d in range(X):
        give_core(d).wait_send()
        keep(d).wait()
    for d in range(X):
        k = 2 * lax.rem(x + d, X) + 1 - c
        remote(wb.at[k], out_rows(k), sd.at[d], rd.at[d], at(cc=1 - c)).wait_recv()


def body(grads, last_peak, master, moment1, moment2):
    f32, bf16 = jnp.float32, jnp.bfloat16
    vmem = lambda *shape, dtype=f32: pltpu.VMEM(shape, dtype)
    dma = lambda n: pltpu.SemaphoreType.DMA((n,))
    own = jax.ShapeDtypeStruct((OWNED, WIDTH), f32)
    updated, first, second, weights, peak = pl.pallas_call(
        kernel,
        out_shape=[
            own, own, own,
            jax.ShapeDtypeStruct((ROWS, WIDTH), bf16),
            jax.ShapeDtypeStruct((LANE_ROWS, WIDTH), f32),
        ],
        in_specs=[pl.BlockSpec(memory_space=pl.ANY)] * 5,
        out_specs=[pl.BlockSpec(memory_space=pl.ANY)] * 5,
        scratch_shapes=[
            vmem(ROWS, WIDTH),
            vmem(LANE_ROWS, WIDTH),
            vmem(3, OWNED, WIDTH),
            vmem(3, OWNED, WIDTH),
            vmem(ROWS, WIDTH, dtype=bf16),
            vmem(X * C, PIECE, WIDTH, dtype=bf16),
            vmem(X * C, 4, WIDTH),
            vmem(X * C, 4, WIDTH),
            vmem(PIECE, WIDTH),
            vmem(8, SHARE, WIDTH),
            vmem(4, 1, WIDTH),
            vmem(Y, SHARE, WIDTH),
            vmem(Y, 1, WIDTH),
            vmem(Z, OWNED, WIDTH),
            vmem(Z, OWNED, WIDTH),
            vmem(1, WIDTH),
            vmem(Z, 1, WIDTH),
            vmem(OWNED, WIDTH),
            vmem(Z, OWNED, WIDTH),
            vmem(SHARE, WIDTH),
            vmem(SHARE, WIDTH, dtype=bf16),
            vmem(8, SHARE, WIDTH, dtype=bf16),
            vmem(Y, 1, WIDTH),
            vmem(PIECE, WIDTH),
            vmem(X * C, PIECE, WIDTH, dtype=bf16),
            vmem(Y, WIDTH),
            vmem(X, Y, WIDTH),
            vmem(LANE_ROWS, WIDTH),
            dma(CHUNKS), dma(4), dma(4),
            dma(8), dma(8), dma(8), dma(8),
            dma(8), dma(8), dma(8), dma(8),
            dma(Z), dma(Z), dma(Z), dma(Z),
            dma(Z), dma(Z), dma(8), dma(8), dma(8), dma(8),
            dma(X), dma(8), dma(X), dma(X), dma(X), dma(X), dma(X),
        ],
        compiler_params=pltpu.CompilerParams(collective_id=0, has_side_effects=True),
    )(grads.reshape(ROWS, WIDTH), last_peak.reshape(LANE_ROWS, WIDTH), master, moment1, moment2)
    return (updated, first, second, weights, peak.reshape(ROWS))


def solution(mesh):
    torus = Mesh(mesh.devices.reshape(X, Y, C, Z), AXES)
    in_specs = (P(AXES, None, None), P(), P(AXES, None), P(AXES, None), P(AXES, None))
    out_specs = (P(AXES, None), P(AXES, None), P(AXES, None), P(), P())
    return jax.shard_map(body, mesh=torus, in_specs=in_specs, out_specs=out_specs, check_vma=False)
```

time: 178 us -> 65.7 us (0.37)
  the two profiles are of different devices: /device:TPU:8 before, /device:TPU:1 now
where the time goes in v1:
time: 65.7 us; the launch traced here: 65.4 us
  Pallas kernels  58.6 us (89%)
  local copies, waits for them, and re-layouts  6.24 us (9%)
    pallas_call x1, Pallas kernels, body(): pl.pallas_call(kernel, out_shape=[own, own, own, jax.ShapeDtypeStruct((RO...  58.6 us
    unnamed x7, local copies, waits for them, and re-layouts  6.24 us

profile of v1, /device:TPU:1, one launch (start us, length us, event | category | flops | bytes accessed | tf_op | source)
XLA Modules:
  0.0 65.4 jit_solution(6720775718801502907)
XLA Ops:
  0.6 58.6 %shard_map.92 = (f32[3,128]{1,0:T(4,128)}, f32[3,128]{1,0:T(4,128)}, f32[3,128]{1,0:T(4,128)}, bf16[2304,128]{1,0:T(8,128)(2,1)}, f32[18,128]{1,0:T(8,128)}) custom-call(f32[2304,128]{1,0:T(8,128)} %bitcast.3, f32[18,128]{1,0:T(8,128)} %bitcast.4, f32[3,128]{1,0:T(4,128)} %master.1, f32[3,128]{1,0:T(4,128)} %moment1.1, f32[3,128]{1,0:T(4,128)} %moment2.1), custom_call_target="tpu_custom_call" | custom-call | tf_op jit(solution)/shard_map/pallas_call | solution.py:434
  59.2 0.0 copy-start
  59.2 1.3 %copy.15 = f32[3,128]{1,0:T(4,128)} copy(f32[3,128]{1,0:T(4,128)} %get-tuple-element.20) | data formatting | bytes 3072
  60.5 1.2 %copy.16 = f32[3,128]{1,0:T(4,128)} copy(f32[3,128]{1,0:T(4,128)} %get-tuple-element.21) | data formatting | bytes 3072
  61.7 1.2 %copy.17 = f32[3,128]{1,0:T(4,128)} copy(f32[3,128]{1,0:T(4,128)} %get-tuple-element.22) | data formatting | bytes 3072
  62.9 1.9 %copy.18 = bf16[2304,128]{1,0:T(8,128)(2,1)} copy(bf16[2304,128]{1,0:T(8,128)(2,1)} %get-tuple-element.23) | data formatting | bytes 1179648
  64.8 0.0 copy-done
  64.8 0.6 copy.19
Async XLA Ops:
  59.2 5.6 %copy-start = (f32[18,128]{1,0:T(8,128)S(1)}, f32[18,128]{1,0:T(8,128)}, u32[]{:S(2)}) copy-start(f32[18,128]{1,0:T(8,128)} %get-tuple-element.14) | copy-start | bytes 27652

commit v2 on v1

v2 whole, which is shorter than its diff:
```python
import functools

import jax
import jax.numpy as jnp
from jax import lax
from jax.experimental import pallas as pl
from jax.experimental.pallas import tpu as pltpu
from jax.sharding import Mesh
from jax.sharding import PartitionSpec as P

STEP_COUNT = 10
AXES = ("dp_0", "dp_1", "dp_2", "fsdp")
MESH = pl.DeviceIdType.MESH

code_limit = 448.0
peak_floor = 0.05
beta_one = 0.9
beta_two = 0.95
learn_rate = 0.05
decay_rate = 0.1
epsilon = 1e-08

X, Y, C, Z = 4, 8, 2, 12
ROWS, WIDTH = 2304, 128
PIECE = ROWS // (X * C)
GROUP = ROWS // (X * Y)
SHARE = GROUP // C
OWNED = SHARE // Z
LANE_ROWS = ROWS // WIDTH


def adamw(gradient, master, moment1, moment2):
    first = beta_one * moment1 + (1.0 - beta_one) * gradient
    second = beta_two * moment2 + (1.0 - beta_two) * gradient * gradient
    corrected_one = first / (1.0 - beta_one**STEP_COUNT)
    corrected_two = second / (1.0 - beta_two**STEP_COUNT)
    updated = master - learn_rate * (
        corrected_one / (jnp.sqrt(corrected_two) + epsilon) + decay_rate * master
    )
    return (updated, first, second)


_cur = [None]


def phase(name):
    if _cur[0] is not None:
        _cur[0].__exit__(None, None, None)
    _cur[0] = None
    if name:
        _cur[0] = jax.named_scope(name)
        _cur[0].__enter__()


def kernel(
    grads, last_peak, master, moment1, moment2,
    stepped, wb, peak_lanes,
    g, lp, inv, state, codes, r1, pk1, rp1, t1, s1, p1, r2, rp2, s2, r3, p3, rp3,
    w3, gz, a36, ay, gy, rp4, t288, pg, rp5,
    up, down, load_sem, small_sem, sem,
    rx,
):
    x, y, c, z = (lax.axis_index(a) for a in AXES)
    mine = 2 * x + c
    half = y // 4
    inside = lax.rem(y, 4)
    far_z = (6, 7, 5, 8, 4, 9, 3, 10, 2, 11, 1)
    far_y = (4, 5, 3, 6, 2, 7, 1)
    far_k = (4, 5, 3, 6, 2, 7, 1)
    count = [0]

    def new_sem():
        count[0] += 1
        return sem.at[count[0] - 1]

    def at(xx=None, yy=None, cc=None, zz=None):
        where = {"dp_0": xx, "dp_1": yy, "dp_2": cc, "fsdp": zz}
        return {k: v for k, v in where.items() if v is not None}

    def signal(semaphore, **where):
        pl.semaphore_signal(semaphore, inc=1, device_id=at(**where), device_id_type=MESH)

    def remote(src, dst, send, recv, where):
        return pltpu.make_async_remote_copy(
            src_ref=src, dst_ref=dst, send_sem=send, recv_sem=recv, device_id=where, device_id_type=MESH
        )

    def arrived(ref, semaphore):
        remote(ref, ref, semaphore, semaphore, at(cc=1 - c)).wait_recv()

    def departed(ref, semaphore):
        remote(ref, ref, semaphore, semaphore, at(cc=1 - c)).wait_send()

    phase("a_signal")
    barrier = pltpu.get_barrier_semaphore()
    signal(barrier, zz=lax.rem(z + 1, Z))
    signal(barrier, zz=lax.rem(z + Z - 1, Z))
    for d in far_y:
        for cc in range(C):
            signal(barrier, yy=lax.rem(y + d, Y), cc=cc)
    for d in (2, 3, 1):
        for cc in range(C):
            signal(barrier, xx=lax.rem(x + d, X), cc=cc)
    signal(barrier, cc=1 - c)

    phase("b_load")
    lp_copy = pltpu.make_async_copy(last_peak, lp, small_sem.at[0])
    lp_copy.start()

    def rows_of(k):
        return pl.ds(pl.multiple_of(k * PIECE, 32), PIECE)

    order = [lax.rem(mine + d, X * C) for d in far_k + (0,)]
    loads = [
        pltpu.make_async_copy(grads.at[rows_of(k)], g.at[rows_of(k)], load_sem.at[i])
        for i, k in enumerate(order)
    ]
    for copy in loads:
        copy.start()
    state_copies = [
        pltpu.make_async_copy(src, state.at[i], small_sem.at[1 + i])
        for i, src in enumerate((master, moment1, moment2))
    ]
    for copy in state_copies:
        copy.start()
    lp_copy.wait()

    phase("c_inverse")
    square = (WIDTH, WIDTH)
    row_at = lax.broadcasted_iota(jnp.int32, square, 0)
    lane_at = lax.broadcasted_iota(jnp.int32, square, 1)
    for r in range(LANE_ROWS):
        inverse = code_limit / jnp.maximum(lp[pl.ds(r, 1), :], peak_floor)
        spread = jnp.where(row_at == lane_at, jnp.broadcast_to(inverse, square), 0.0)
        column = jnp.sum(spread, axis=1, keepdims=True)
        inv[pl.ds(r * WIDTH, WIDTH), :] = jnp.broadcast_to(column, square)

    def encode(i):
        loads[i].wait()
        rows = rows_of(order[i])
        codes[rows, :] = jnp.clip(g[rows, :] * inv[rows, :], -code_limit, code_limit).astype(jnp.bfloat16)

    phase("d_first")
    encode(0)

    phase("e_barrier")
    pl.semaphore_wait(barrier, 2 + (Y - 1) * C + (X - 1) * C + 1)

    phase("f_send1")
    sent_codes, got_codes, sent_pk1, got_pk1 = (new_sem() for _ in range(4))
    for i, k in enumerate(order[:-1]):
        if i:
            encode(i)
        remote(codes.at[rows_of(k)], r1.at[mine], sent_codes, got_codes, at(xx=k // 2, cc=lax.rem(k, 2))).start()
    encode(X * C - 1)

    phase("g_zround")

    def tell(upwards, downwards):
        signal(up, zz=lax.rem(z + 1, Z))
        signal(down, zz=lax.rem(z + Z - 1, Z))

    def hear():
        pl.semaphore_wait(up, 1)
        pl.semaphore_wait(down, 1)

    tell(up, down)

    phase("h_peaks")
    tall = (GROUP, WIDTH)
    tall_row = lax.broadcasted_iota(jnp.int32, tall, 0)
    tall_lane = lax.broadcasted_iota(jnp.int32, tall, 1)
    for k in range(X * C):
        for i in range(4):
            rows = pl.ds((4 * k + i) * GROUP, GROUP)
            top = jnp.max(jnp.abs(g[rows, :]), axis=1, keepdims=True)
            laid = jnp.where(tall_row == tall_lane, jnp.broadcast_to(top, tall), 0.0)
            pk1[k, i : i + 1, :] = jnp.max(laid, axis=0, keepdims=True)
    for k in order[:-1]:
        remote(pk1.at[k], rp1.at[mine], sent_pk1, got_pk1, at(xx=k // 2, cc=lax.rem(k, 2))).start()

    phase("i_zround")
    for _ in range(Z // 2 - 2):
        hear()
        tell(up, down)
    hear()

    phase("j_scale")
    first_row = (((x * Y + y) * C + c) * Z + z) * OWNED
    flat = lax.broadcasted_iota(jnp.int32, (LANE_ROWS, WIDTH), 0) * WIDTH + lax.broadcasted_iota(
        jnp.int32, (LANE_ROWS, WIDTH), 1
    )
    own_row = lax.broadcasted_iota(jnp.int32, (OWNED, WIDTH), 0)
    all_scales = jnp.maximum(lp[...], peak_floor) / code_limit
    scale = jnp.zeros((OWNED, WIDTH), jnp.float32)
    for j in range(OWNED):
        one = jnp.sum(jnp.where(flat == first_row + j, all_scales, 0.0), axis=(0, 1), keepdims=True)
        scale = jnp.where(own_row == j, jnp.broadcast_to(one, scale.shape), scale)

    phase("k_wait1")
    arrived(r1.at[pl.ds(0, X * C - 1)], got_codes)

    phase("l_sum1")
    block = 48
    for b in range(PIECE // block):
        own = codes[pl.ds(pl.multiple_of(mine * PIECE + b * block, 16), block), :]
        total = own.astype(jnp.float32)
        for d in range(1, X * C):
            k = lax.rem(mine + d, X * C)
            total = total + r1[k, pl.ds(b * block, block), :].astype(jnp.float32)
        t1[pl.ds(b * block, block), :] = total
    for m in range(8):
        s1[m] = t1[pl.ds(m * SHARE, SHARE), :]

    phase("m_send2")
    sent2, got2, sent_p2, got_p2 = (new_sem() for _ in range(4))
    local = half == c

    def to_y(start, source, landing, semaphores):
        for d in (2, 3, 1):
            for cc in range(C):
                i = lax.rem(inside + d, 4)
                start(source(i, cc), landing, semaphores, at(yy=4 * c + i, cc=cc))
        start(source(inside, 1 - c), landing, semaphores, at(yy=4 * c + inside, cc=1 - c))

        @pl.when(jnp.logical_not(local))
        def _():
            start(source(inside, c), landing, semaphores, at(yy=4 * c + inside, cc=c))

    def start(src, dst, semaphores, where):
        remote(src, dst, *semaphores, where).start()

    def finish(kind, ref, semaphore):
        @pl.when(local)
        def _():
            kind(ref.at[pl.ds(0, 7)], semaphore)

        @pl.when(jnp.logical_not(local))
        def _():
            kind(ref, semaphore)

    to_y(start, lambda i, cc: s1.at[2 * i + cc], r2.at[y], (sent2, got2))

    @pl.when(local)
    def _():
        r2[y] = s1[2 * inside + c]

    phase("n_peak1")
    arrived(rp1.at[pl.ds(0, X * C - 1)], got_pk1)
    top = pk1[mine]
    for d in range(1, X * C):
        top = jnp.maximum(top, rp1[lax.rem(mine + d, X * C)])
    for i in range(4):
        p1[i] = top[i : i + 1, :]
    to_y(start, lambda i, cc: p1.at[i], rp2.at[y], (sent_p2, got_p2))

    @pl.when(local)
    def _():
        rp2[y] = p1[inside]

    phase("o_wait2")
    finish(arrived, r2, got2)
    phase("p_sum2")
    total = r2[0]
    for i in range(1, Y):
        total = total + r2[i]
    for i in range(Z):
        s2[i] = total[i * OWNED : (i + 1) * OWNED, :]

    phase("q_send3")
    sent3, got3, sent_p3, got_p3 = (new_sem() for _ in range(4))
    for d in far_z:
        zz = lax.rem(z + d, Z)
        start(s2.at[zz], r3.at[z], (sent3, got3), at(zz=zz))

    phase("r_peak2")
    finish(arrived, rp2, got_p2)
    top = rp2[0]
    for i in range(1, Y):
        top = jnp.maximum(top, rp2[i])
    p3[...] = top
    for d in far_z:
        start(p3, rp3.at[z], (sent_p3, got_p3), at(zz=lax.rem(z + d, Z)))

    for copy in state_copies:
        copy.wait()
    phase("s_wait3")
    arrived(r3.at[pl.ds(0, Z - 1)], got3)
    phase("t_adam")
    total = s2[z]
    for d in range(1, Z):
        total = total + r3[lax.rem(z + d, Z)]
    gradient = total * scale
    updated, first, second = adamw(gradient, state[0], state[1], state[2])
    w3[...] = updated.astype(jnp.bfloat16).astype(jnp.float32)

    phase("u_givez")
    sent_z, got_z = new_sem(), new_sem()
    for d in far_z:
        start(w3, gz.at[z], (sent_z, got_z), at(zz=lax.rem(z + d, Z)))
    gz[z] = w3[...]
    stepped[0] = updated
    stepped[1] = first
    stepped[2] = second

    phase("v_peak3")
    arrived(rp3.at[pl.ds(0, Z - 1)], got_p3)
    top = p3[...]
    for d in range(1, Z):
        top = jnp.maximum(top, rp3[lax.rem(z + d, Z)])
    rp4[y] = top
    sent_p4, got_p4 = new_sem(), new_sem()
    for d in far_y:
        start(rp4.at[y], rp4.at[y], (sent_p4, got_p4), at(yy=lax.rem(y + d, Y)))

    phase("w_waitgz")
    arrived(gz.at[pl.ds(0, Z - 1)], got_z)
    phase("x_asm36")
    for i in range(Z):
        a36[pl.ds(i * OWNED, OWNED), :] = gz[i]
    ay[...] = a36[...].astype(jnp.bfloat16)

    phase("y_givey")
    slot = 2 * inside + c
    sent_y, got_y = new_sem(), new_sem()
    for d in far_y:
        start(ay, gy.at[slot], (sent_y, got_y), at(yy=lax.rem(y + d, Y), cc=half))

    @pl.when(jnp.logical_not(local))
    def _():
        start(ay, gy.at[slot], (sent_y, got_y), at(cc=half))

    @pl.when(local)
    def _():
        gy[slot] = ay[...]

    phase("z_peakx")
    arrived(rp4.at[pl.ds(0, Y - 1)], got_p4)
    for i in range(Y):
        pg[i : i + 1, :] = rp4[i]
    sent_p5, got_p5 = new_sem(), new_sem()
    for d in (2, 3, 1):
        start(pg, rp5.at[x], (sent_p5, got_p5), at(xx=lax.rem(x + d, X)))
    rp5[x] = pg[...]

    phase("za_waitgy")
    finish(arrived, gy, got_y)
    phase("zb_asm288")
    for m in range(8):
        t288[pl.ds(m * SHARE, SHARE), :] = gy[m].astype(jnp.float32)
    wb[rows_of(mine), :] = t288[...].astype(jnp.bfloat16)

    phase("zc_givex")
    sent_x, sent_core, got_core = (new_sem() for _ in range(3))
    own_piece = wb.at[rows_of(mine)]
    for d in (2, 3, 1):
        start(own_piece, own_piece, (sent_x, rx.at[x]), at(xx=lax.rem(x + d, X)))

    def give_core(xx):
        piece = wb.at[rows_of(2 * xx + c)]
        start(piece, piece, (sent_core, got_core), at(cc=1 - c))

    give_core(x)

    phase("zd_peaks")
    arrived(rp5.at[pl.ds(0, X - 1)], got_p5)
    lane_of = lax.broadcasted_iota(jnp.int32, (1, WIDTH), 1)
    for j in range(LANE_ROWS):
        line = jnp.zeros((1, WIDTH), jnp.float32)
        for n in range(X * Y):
            lo = GROUP * n - WIDTH * j
            if lo >= WIDTH or lo + GROUP <= 0:
                continue
            row = rp5[n // Y, n % Y : n % Y + 1, :]
            if lo % WIDTH:
                row = pltpu.roll(row, lo % WIDTH, 1)
            line = jnp.where((lane_of >= lo) & (lane_of < lo + GROUP), row, line)
        peak_lanes[j : j + 1, :] = line

    phase("ze_waitgx")
    for d in (1, 3, 2):
        xx = lax.rem(x + d, X)
        arrived(wb.at[rows_of(2 * xx + c)], rx.at[xx])
        give_core(xx)

    phase("zf_drain")
    departed(r1.at[pl.ds(0, X * C - 1)], sent_codes)
    departed(rp1.at[pl.ds(0, X * C - 1)], sent_pk1)
    finish(departed, r2, sent2)
    finish(departed, rp2, sent_p2)
    departed(r3.at[pl.ds(0, Z - 1)], sent3)
    departed(rp3.at[pl.ds(0, Z - 1)], sent_p3)
    departed(gz.at[pl.ds(0, Z - 1)], sent_z)
    departed(rp4.at[pl.ds(0, Y - 1)], sent_p4)
    finish(departed, gy, sent_y)
    departed(rp5.at[pl.ds(0, X - 1)], sent_p5)
    departed(r1.at[pl.ds(0, X - 1)], sent_x)
    departed(r1.at[pl.ds(0, X)], sent_core)
    arrived(r1.at[pl.ds(0, X)], got_core)
    phase(None)


SEMS = 24


def store(stepped, wb, peak_lanes, out_master, out_first, out_second, weights, out_peak, sem):
    copies = [pltpu.make_async_copy(wb, weights, sem.at[0])]
    for i, dst in enumerate((out_master, out_first, out_second)):
        copies.append(pltpu.make_async_copy(stepped.at[i], dst, sem.at[1 + i]))
    copies.append(pltpu.make_async_copy(peak_lanes, out_peak, sem.at[4]))
    for copy in copies:
        copy.start()
    for copy in copies:
        copy.wait()


def body(grads, last_peak, master, moment1, moment2):
    f32, bf16 = jnp.float32, jnp.bfloat16
    vmem = lambda *shape, dtype=f32: pltpu.VMEM(shape, dtype)
    dma = lambda n: pltpu.SemaphoreType.DMA((n,))
    own = jax.ShapeDtypeStruct((OWNED, WIDTH), f32)
    whole = jax.ShapeDtypeStruct((ROWS, WIDTH), bf16)
    lanes = jax.ShapeDtypeStruct((LANE_ROWS, WIDTH), f32)
    in_vmem = pl.BlockSpec(memory_space=pltpu.VMEM)
    anywhere = pl.BlockSpec(memory_space=pl.ANY)
    held = pl.pallas_call(
        kernel,
        out_shape=[jax.ShapeDtypeStruct((3, OWNED, WIDTH), f32), whole, lanes],
        in_specs=[pl.BlockSpec(memory_space=pltpu.HBM)] * 5,
        out_specs=[in_vmem] * 3,
        scratch_shapes=[
            vmem(ROWS, WIDTH),
            vmem(LANE_ROWS, WIDTH),
            vmem(ROWS, WIDTH),
            vmem(3, OWNED, WIDTH),
            vmem(ROWS, WIDTH, dtype=bf16),
            vmem(X * C, PIECE, WIDTH, dtype=bf16),
            vmem(X * C, 4, WIDTH),
            vmem(X * C, 4, WIDTH),
            vmem(PIECE, WIDTH),
            vmem(8, SHARE, WIDTH),
            vmem(4, 1, WIDTH),
            vmem(Y, SHARE, WIDTH),
            vmem(Y, 1, WIDTH),
            vmem(Z, OWNED, WIDTH),
            vmem(Z, OWNED, WIDTH),
            vmem(1, WIDTH),
            vmem(Z, 1, WIDTH),
            vmem(OWNED, WIDTH),
            vmem(Z, OWNED, WIDTH),
            vmem(SHARE, WIDTH),
            vmem(SHARE, WIDTH, dtype=bf16),
            vmem(8, SHARE, WIDTH, dtype=bf16),
            vmem(Y, 1, WIDTH),
            vmem(PIECE, WIDTH),
            vmem(Y, WIDTH),
            vmem(X, Y, WIDTH),
            pltpu.SemaphoreType.REGULAR,
            pltpu.SemaphoreType.REGULAR,
            dma(X * C), dma(4), dma(SEMS), dma(X),
        ],
        compiler_params=pltpu.CompilerParams(
            collective_id=0, has_side_effects=True, vmem_limit_bytes=16 * 2**20
        ),
    )(*(
        pltpu.with_memory_space_constraint(a, pltpu.HBM)
        for a in (grads.reshape(ROWS, WIDTH), last_peak.reshape(LANE_ROWS, WIDTH), master, moment1, moment2)
    ))
    updated, first, second, weights, peak = pl.pallas_call(
        store,
        out_shape=[own, own, own, whole, lanes],
        in_specs=[in_vmem] * 3,
        out_specs=[anywhere] * 5,
        scratch_shapes=[dma(5)],
        compiler_params=pltpu.CompilerParams(vmem_limit_bytes=8 * 2**20),
    )(*held)
    return (updated, first, second, weights, peak.reshape(ROWS))


def solution(mesh):
    torus = Mesh(mesh.devices.reshape(X, Y, C, Z), AXES)
    in_specs = (P(AXES, None, None), P(), P(AXES, None), P(AXES, None), P(AXES, None))
    out_specs = (P(AXES, None), P(AXES, None), P(AXES, None), P(), P())
    return jax.shard_map(body, mesh=torus, in_specs=in_specs, out_specs=out_specs, check_vma=False)
```

time: 65.7 us -> 58.3 us (0.89)
  local copies, waits for them, and re-layouts: 6.24 us -> 0 us
  Pallas kernels: 58.6 us -> 57.5 us
    unnamed x7 -> x0, local copies, waits for them, and re-layouts: 6.24 us -> none
    pallas_call x1 -> x2, Pallas kernels: 58.6 us -> 57.5 us  [the longest x1 56.6 us: body(): pl.pallas_call(kernel, out_shape=[jax.ShapeDtypeStruct((3, OWNED, WIDTH),...]
where the time goes in v2:
time: 58.3 us; the launch traced here: 58.1 us
  Pallas kernels  57.5 us (99%)
  between operations  0.64 us (1%)
    pallas_call x1, Pallas kernels, body(): pl.pallas_call(kernel, out_shape=[jax.ShapeDtypeStruct((3, OWNED, WIDTH),...  56.6 us

profile of v2, /device:TPU:1, one launch (start us, length us, event | category | flops | bytes accessed | tf_op | source)
XLA Modules:
  0.0 58.1 jit_solution(6188115764644931375)
XLA Ops:
  0.6 56.6 %shard_map.92 = (f32[3,3,128]{2,1,0:T(4,128)S(1)}, bf16[2304,128]{1,0:T(8,128)(2,1)S(1)}, f32[18,128]{1,0:T(8,128)S(1)}) custom-call(f32[2304,128]{1,0:T(8,128)} %bitcast.3, f32[18,128]{1,0:T(8,128)} %bitcast.4, f32[3,128]{1,0:T(4,128)} %master.1, f32[3,128]{1,0:T(4,128)} %moment1.1, f32[3,128]{1,0:T(4,128)} %moment2.1), custom_call_target="tpu_custom_call" | custom-call | tf_op jit(solution)/shard_map/pallas_call | solution.py:426
  57.3 0.9 %shard_map.93 = (f32[3,128]{1,0:T(4,128)}, f32[3,128]{1,0:T(4,128)}, f32[3,128]{1,0:T(4,128)}, bf16[2304,128]{1,0:T(8,128)(2,1)}, f32[18,128]{1,0:T(8,128)}) custom-call(f32[3,3,128]{2,1,0:T(4,128)S(1)} %get-tuple-element.13.stepped, bf16[2304,128]{1,0:T(8,128)(2,1)S(1)} %get-tuple-element.14.wb, f32[18,128]{1,0:T(8,128)S(1)} %get-tuple-element.15.peak_lanes), custom_call_target="tpu_custom_call" | custom-call | tf_op jit(solution)/shard_map/pallas_call | solution.py:469

commit v3 on v2

--- a/solution.py
+++ b/solution.py
@@ -27,6 +27,10 @@
 SHARE = GROUP // C
 OWNED = SHARE // Z
 LANE_ROWS = ROWS // WIDTH
+FIRST = 40
+LAST = GROUP - FIRST
+SPLIT = FIRST - SHARE
+NEAR = 3
 
 
 def adamw(gradient, master, moment1, moment2):
@@ -55,15 +59,19 @@
 def kernel(
     grads, last_peak, master, moment1, moment2,
     stepped, wb, peak_lanes,
-    g, lp, inv, state, codes, r1, pk1, rp1, t1, s1, p1, r2, rp2, s2, r3, p3, rp3,
-    w3, gz, a36, ay, gy, rp4, t288, pg, rp5,
-    up, down, load_sem, small_sem, sem,
-    rx,
+    g, lp, inv, state, codes_a, codes_b, r1a, r1b, pk1, rp1, s1a, s1b, s1c, p1, r2a, r2b, r2c, rp2, t36,
+    s2, r3, p3, rp3, w3, gz, a36, ay, a4, b32, gya, gyb, rp4, t160, pg, rp5,
+    up, down, load_sem, small_sem, sem, rxa, ryb,
 ):
     x, y, c, z = (lax.axis_index(a) for a in AXES)
     mine = 2 * x + c
     half = y // 4
     inside = lax.rem(y, 4)
+    xhalf = x // 2
+    xin = lax.rem(x, 2)
+    first_core = c == 0
+    last_core = c == 1
+    local = half == c
     far_z = (6, 7, 5, 8, 4, 9, 3, 10, 2, 11, 1)
     far_y = (4, 5, 3, 6, 2, 7, 1)
     far_k = (4, 5, 3, 6, 2, 7, 1)
@@ -93,8 +101,9 @@
 
     phase("a_signal")
     barrier = pltpu.get_barrier_semaphore()
-    signal(barrier, zz=lax.rem(z + 1, Z))
-    signal(barrier, zz=lax.rem(z + Z - 1, Z))
+    for d in range(NEAR, 0, -1):
+        signal(barrier, zz=lax.rem(z + d, Z))
+        signal(barrier, zz=lax.rem(z + Z - d, Z))
     for d in far_y:
         for cc in range(C):
             signal(barrier, yy=lax.rem(y + d, Y), cc=cc)
@@ -107,12 +116,13 @@
     lp_copy = pltpu.make_async_copy(last_peak, lp, small_sem.at[0])
     lp_copy.start()
 
-    def rows_of(k):
-        return pl.ds(pl.multiple_of(k * PIECE, 32), PIECE)
-
     order = [lax.rem(mine + d, X * C) for d in far_k + (0,)]
     loads = [
-        pltpu.make_async_copy(grads.at[rows_of(k)], g.at[rows_of(k)], load_sem.at[i])
+        pltpu.make_async_copy(
+            grads.at[pl.ds(pl.multiple_of(k * PIECE, 32), PIECE)],
+            g.at[pl.ds(pl.multiple_of(k * PIECE, 32), PIECE)],
+            load_sem.at[i],
+        )
         for i, k in enumerate(order)
     ]
     for copy in loads:
@@ -135,36 +145,52 @@
         column = jnp.sum(spread, axis=1, keepdims=True)
         inv[pl.ds(r * WIDTH, WIDTH), :] = jnp.broadcast_to(column, square)
 
+    def scaled(at_row, count):
+        rows = pl.ds(pl.multiple_of(at_row, 8), count)
+        return jnp.clip(g[rows, :] * inv[rows, :], -code_limit, code_limit)
+
     def encode(i):
         loads[i].wait()
-        rows = rows_of(order[i])
-        codes[rows, :] = jnp.clip(g[rows, :] * inv[rows, :], -code_limit, code_limit).astype(jnp.bfloat16)
+        k = order[i]
+        xx, cc = k // 2, lax.rem(k, 2)
+        for n in range(2):
+            pair = [scaled((4 * k + 2 * n + m) * GROUP, FIRST) for m in range(2)]
+            codes_a[k, pl.ds(2 * n * FIRST, 2 * FIRST), :] = jnp.concatenate(pair, axis=0).astype(jnp.bfloat16)
+        for n in range(4):
+            codes_b[xx, 4 * cc + n] = scaled((4 * k + n) * GROUP + FIRST, LAST).astype(jnp.bfloat16)
 
     phase("d_first")
     encode(0)
 
     phase("e_barrier")
-    pl.semaphore_wait(barrier, 2 + (Y - 1) * C + (X - 1) * C + 1)
+    pl.semaphore_wait(barrier, 2 * NEAR + (Y - 1) * C + (X - 1) * C + 1)
 
     phase("f_send1")
-    sent_codes, got_codes, sent_pk1, got_pk1 = (new_sem() for _ in range(4))
-    for i, k in enumerate(order[:-1]):
+    mine_y = 2 * y + c
+    sent_1a, got_1a, sent_1b, got_1b, sent_pk1, got_pk1 = (new_sem() for _ in range(6))
+
+    def start(src, dst, semaphores, where):
+        remote(src, dst, *semaphores, where).start()
+
+    for i, k in enumerate(order):
         if i:
             encode(i)
-        remote(codes.at[rows_of(k)], r1.at[mine], sent_codes, got_codes, at(xx=k // 2, cc=lax.rem(k, 2))).start()
-    encode(X * C - 1)
+        xx, cc = k // 2, lax.rem(k, 2)
+        if i < X * C - 1:
+            start(codes_a.at[k], r1a.at[mine], (sent_1a, got_1a), at(xx=xx, cc=cc))
+        reader = xx // 2
+        for n in (2, 3, 1):
+            yy = 4 * cc + lax.rem(inside + n, 4)
+            start(codes_b.at[xx, yy], r1b.at[mine_y, lax.rem(xx, 2)], (sent_1b, got_1b), at(yy=yy, cc=reader))
+        yy = 4 * cc + inside
+
+        @pl.when((yy != y) | (reader != c))
+        def _(xx=xx, yy=yy, reader=reader):
+            start(codes_b.at[xx, yy], r1b.at[mine_y, lax.rem(xx, 2)], (sent_1b, got_1b), at(yy=yy, cc=reader))
 
     phase("g_zround")
-
-    def tell(upwards, downwards):
-        signal(up, zz=lax.rem(z + 1, Z))
-        signal(down, zz=lax.rem(z + Z - 1, Z))
-
-    def hear():
-        pl.semaphore_wait(up, 1)
-        pl.semaphore_wait(down, 1)
-
-    tell(up, down)
+    signal(up, zz=lax.rem(z + NEAR, Z))
+    signal(down, zz=lax.rem(z + Z - NEAR, Z))
 
     phase("h_peaks")
     tall = (GROUP, WIDTH)
@@ -179,12 +205,6 @@
     for k in order[:-1]:
         remote(pk1.at[k], rp1.at[mine], sent_pk1, got_pk1, at(xx=k // 2, cc=lax.rem(k, 2))).start()
 
-    phase("i_zround")
-    for _ in range(Z // 2 - 2):
-        hear()
-        tell(up, down)
-    hear()
-
     phase("j_scale")
     first_row = (((x * Y + y) * C + c) * Z + z) * OWNED
     flat = lax.broadcasted_iota(jnp.int32, (LANE_ROWS, WIDTH), 0) * WIDTH + lax.broadcasted_iota(
@@ -197,53 +217,62 @@
         one = jnp.sum(jnp.where(flat == first_row + j, all_scales, 0.0), axis=(0, 1), keepdims=True)
         scale = jnp.where(own_row == j, jnp.broadcast_to(one, scale.shape), scale)
 
-    phase("k_wait1")
-    arrived(r1.at[pl.ds(0, X * C - 1)], got_codes)
-
-    phase("l_sum1")
-    block = 48
-    for b in range(PIECE // block):
-        own = codes[pl.ds(pl.multiple_of(mine * PIECE + b * block, 16), block), :]
-        total = own.astype(jnp.float32)
+    def either(condition, kind, ref, semaphore, fewer, more):
+        @pl.when(condition)
+        def _():
+            kind(ref.at[pl.ds(0, fewer)], semaphore)
+
+        @pl.when(jnp.logical_not(condition))
+        def _():
+            kind(ref.at[pl.ds(0, more)], semaphore)
+
+    phase("k_wait1a")
+    arrived(r1a.at[pl.ds(0, X * C - 1)], got_1a)
+
+    phase("l_sum1a")
+    block = 80
+    for n in range(2):
+        total = codes_a[mine, pl.ds(n * block, block), :].astype(jnp.float32)
         for d in range(1, X * C):
             k = lax.rem(mine + d, X * C)
-            total = total + r1[k, pl.ds(b * block, block), :].astype(jnp.float32)
-        t1[pl.ds(b * block, block), :] = total
-    for m in range(8):
-        s1[m] = t1[pl.ds(m * SHARE, SHARE), :]
-
-    phase("m_send2")
-    sent2, got2, sent_p2, got_p2 = (new_sem() for _ in range(4))
-    local = half == c
-
-    def to_y(start, source, landing, semaphores):
+            total = total + r1a[k, pl.ds(n * block, block), :].astype(jnp.float32)
+        for m in range(2):
+            s1a[2 * n + m] = total[m * FIRST : m * FIRST + SHARE, :]
+            s1b[2 * n + m] = total[m * FIRST + SHARE : (m + 1) * FIRST, :]
+
+    phase("m_send2a")
+    sent_2a, got_2a, sent_2b, got_2b, sent_p2, got_p2 = (new_sem() for _ in range(6))
+    for d in (2, 3, 1):
+        i = lax.rem(inside + d, 4)
+        start(s1a.at[i], r2a.at[y], (sent_2a, got_2a), at(yy=4 * c + i, cc=0))
+        start(s1b.at[i], r2b.at[y], (sent_2b, got_2b), at(yy=4 * c + i, cc=1))
+
+    @pl.when(local & first_core)
+    def _():
+        r2a[y] = s1a[inside]
+
+    @pl.when(jnp.logical_not(local & first_core))
+    def _():
+        start(s1a.at[inside], r2a.at[y], (sent_2a, got_2a), at(yy=4 * c + inside, cc=0))
+
+    @pl.when(local & last_core)
+    def _():
+        r2b[y] = s1b[inside]
+
+    @pl.when(jnp.logical_not(local & last_core))
+    def _():
+        start(s1b.at[inside], r2b.at[y], (sent_2b, got_2b), at(yy=4 * c + inside, cc=1))
+
+    def to_y(source, landing, semaphores):
         for d in (2, 3, 1):
             for cc in range(C):
                 i = lax.rem(inside + d, 4)
-                start(source(i, cc), landing, semaphores, at(yy=4 * c + i, cc=cc))
-        start(source(inside, 1 - c), landing, semaphores, at(yy=4 * c + inside, cc=1 - c))
+                start(source.at[i], landing, semaphores, at(yy=4 * c + i, cc=cc))
+        start(source.at[inside], landing, semaphores, at(yy=4 * c + inside, cc=1 - c))
 
         @pl.when(jnp.logical_not(local))
         def _():
-            start(source(inside, c), landing, semaphores, at(yy=4 * c + inside, cc=c))
-
-    def start(src, dst, semaphores, where):
-        remote(src, dst, *semaphores, where).start()
-
-    def finish(kind, ref, semaphore):
-        @pl.when(local)
-        def _():
-            kind(ref.at[pl.ds(0, 7)], semaphore)
-
-        @pl.when(jnp.logical_not(local))
-        def _():
-            kind(ref, semaphore)
-
-    to_y(start, lambda i, cc: s1.at[2 * i + cc], r2.at[y], (sent2, got2))
-
-    @pl.when(local)
-    def _():
-        r2[y] = s1[2 * inside + c]
+            start(source.at[inside], landing, semaphores, at(yy=4 * c + inside, cc=c))
 
     phase("n_peak1")
     arrived(rp1.at[pl.ds(0, X * C - 1)], got_pk1)
@@ -252,29 +281,72 @@
         top = jnp.maximum(top, rp1[lax.rem(mine + d, X * C)])
     for i in range(4):
         p1[i] = top[i : i + 1, :]
-    to_y(start, lambda i, cc: p1.at[i], rp2.at[y], (sent_p2, got_p2))
+    to_y(p1, rp2.at[y], (sent_p2, got_p2))
 
     @pl.when(local)
     def _():
         rp2[y] = p1[inside]
 
-    phase("o_wait2")
-    finish(arrived, r2, got2)
-    phase("p_sum2")
-    total = r2[0]
-    for i in range(1, Y):
-        total = total + r2[i]
+    phase("o_wait1b")
+    arrived(r1b.at[pl.ds(0, Y * C - 1)], got_1b)
+    phase("p_sum1b")
+    for j in range(2):
+        total = codes_b[2 * c + j, y].astype(jnp.float32)
+        for d in range(1, Y * C):
+            total = total + r1b[lax.rem(mine_y + d, Y * C), j].astype(jnp.float32)
+        s1c[j] = total
+    sent_2c, got_2c = new_sem(), new_sem()
+    own_c = (xhalf == c) & last_core
+    i = 1 - xin
+    start(s1c.at[i], r2c.at[x], (sent_2c, got_2c), at(xx=2 * c + i, cc=1))
+
+    @pl.when(own_c)
+    def _():
+        r2c[x] = s1c[xin]
+
+    @pl.when(jnp.logical_not(own_c))
+    def _():
+        start(s1c.at[xin], r2c.at[x], (sent_2c, got_2c), at(xx=2 * c + xin, cc=1))
+
+    phase("pa_zround")
+    pl.semaphore_wait(up, 1)
+    pl.semaphore_wait(down, 1)
+
+    phase("pb_wait2")
+
+    @pl.when(first_core)
+    def _():
+        either(local, arrived, r2a, got_2a, Y - 1, Y)
+        total = r2a[0]
+        for i in range(1, Y):
+            total = total + r2a[i]
+        t36[...] = total
+
+    @pl.when(last_core)
+    def _():
+        either(local, arrived, r2b, got_2b, Y - 1, Y)
+        total = r2b[0]
+        for i in range(1, Y):
+            total = total + r2b[i]
+        t36[0:SPLIT, :] = total
+        either(xhalf == c, arrived, r2c, got_2c, X - 1, X)
+        total = r2c[0]
+        for i in range(1, X):
+            total = total + r2c[i]
+        t36[SPLIT:SHARE, :] = total
+
+    phase("pc_sum2")
     for i in range(Z):
-        s2[i] = total[i * OWNED : (i + 1) * OWNED, :]
+        s2[i] = t36[i * OWNED : (i + 1) * OWNED, :]
 
     phase("q_send3")
-    sent3, got3, sent_p3, got_p3 = (new_sem() for _ in range(4))
+    sent_3, got_3, sent_p3, got_p3 = (new_sem() for _ in range(4))
     for d in far_z:
         zz = lax.rem(z + d, Z)
-        start(s2.at[zz], r3.at[z], (sent3, got3), at(zz=zz))
+        start(s2.at[zz], r3.at[z], (sent_3, got_3), at(zz=zz))
 
     phase("r_peak2")
-    finish(arrived, rp2, got_p2)
+    either(local, arrived, rp2, got_p2, Y - 1, Y)
     top = rp2[0]
     for i in range(1, Y):
         top = jnp.maximum(top, rp2[i])
@@ -285,7 +357,7 @@
     for copy in state_copies:
         copy.wait()
     phase("s_wait3")
-    arrived(r3.at[pl.ds(0, Z - 1)], got3)
+    arrived(r3.at[pl.ds(0, Z - 1)], got_3)
     phase("t_adam")
     total = s2[z]
     for d in range(1, Z):
@@ -319,20 +391,50 @@
     for i in range(Z):
         a36[pl.ds(i * OWNED, OWNED), :] = gz[i]
     ay[...] = a36[...].astype(jnp.bfloat16)
+    a4[...] = a36[0:SPLIT, :]
 
     phase("y_givey")
-    slot = 2 * inside + c
-    sent_y, got_y = new_sem(), new_sem()
-    for d in far_y:
-        start(ay, gy.at[slot], (sent_y, got_y), at(yy=lax.rem(y + d, Y), cc=half))
-
-    @pl.when(jnp.logical_not(local))
-    def _():
-        start(ay, gy.at[slot], (sent_y, got_y), at(cc=half))
-
-    @pl.when(local)
-    def _():
-        gy[slot] = ay[...]
+    sent_ya, got_ya, sent_yb, got_yb, sent_xb, got_xb = (new_sem() for _ in range(6))
+
+    def rows_b(xx, yy):
+        return wb.at[xx, yy, pl.ds(FIRST, LAST)]
+
+    @pl.when(last_core)
+    def _():
+        b32[...] = a36[SPLIT:SHARE, :].astype(jnp.bfloat16)
+        for d in far_y:
+            start(a4, gyb.at[inside], (sent_yb, got_yb), at(yy=lax.rem(y + d, Y), cc=half))
+        for d in (2, 3, 1):
+            start(b32, rows_b(x, y), (sent_xb, got_xb), at(xx=lax.rem(x + d, X), cc=xhalf))
+
+        @pl.when(xhalf == 0)
+        def _():
+            start(b32, rows_b(x, y), (sent_xb, got_xb), at(cc=0))
+
+        @pl.when(xhalf == 1)
+        def _():
+            wb[x, y, pl.ds(FIRST, LAST), :] = b32[...]
+
+        @pl.when(local)
+        def _():
+            gyb[inside] = a4[...]
+
+        @pl.when(jnp.logical_not(local))
+        def _():
+            start(a4, gyb.at[inside], (sent_yb, got_yb), at(cc=0))
+
+    @pl.when(first_core)
+    def _():
+        for d in far_y:
+            start(ay, gya.at[inside], (sent_ya, got_ya), at(yy=lax.rem(y + d, Y), cc=half))
+
+        @pl.when(local)
+        def _():
+            gya[inside] = ay[...]
+
+        @pl.when(jnp.logical_not(local))
+        def _():
+            start(ay, gya.at[inside], (sent_ya, got_ya), at(cc=1))
 
     phase("z_peakx")
     arrived(rp4.at[pl.ds(0, Y - 1)], got_p4)
@@ -343,24 +445,35 @@
         start(pg, rp5.at[x], (sent_p5, got_p5), at(xx=lax.rem(x + d, X)))
     rp5[x] = pg[...]
 
-    phase("za_waitgy")
-    finish(arrived, gy, got_y)
-    phase("zb_asm288")
-    for m in range(8):
-        t288[pl.ds(m * SHARE, SHARE), :] = gy[m].astype(jnp.float32)
-    wb[rows_of(mine), :] = t288[...].astype(jnp.bfloat16)
-
-    phase("zc_givex")
-    sent_x, sent_core, got_core = (new_sem() for _ in range(3))
-    own_piece = wb.at[rows_of(mine)]
+    phase("za_waitxb")
+    sent_x, sent_yc, sent_core, got_core = (new_sem() for _ in range(4))
+    either(own_c, arrived, r1b.at[0], got_xb, 1, 2)
+
+    def part_b(yy):
+        return wb.at[pl.ds(2 * c, 2), yy, pl.ds(FIRST, LAST)]
+
+    for d in far_y:
+        start(part_b(y), part_b(y), (sent_yc, ryb.at[y]), at(yy=lax.rem(y + d, Y)))
+    start(part_b(y), part_b(y), (sent_core, got_core), at(cc=1 - c))
+
+    phase("zb_waitya")
+    either(local & first_core, arrived, gya, got_ya, 3, 4)
+    either(local & last_core, arrived, gyb, got_yb, 3, 4)
+    phase("zc_asm160")
+    for i in range(4):
+        t160[i * FIRST : i * FIRST + SHARE, :] = gya[i].astype(jnp.float32)
+        t160[i * FIRST + SHARE : (i + 1) * FIRST, :] = gyb[i]
+    for i in range(4):
+        wb[x, 4 * c + i, pl.ds(0, FIRST), :] = t160[i * FIRST : (i + 1) * FIRST, :].astype(jnp.bfloat16)
+
+    phase("zd_givex")
+
+    def part_a(xx):
+        return wb.at[xx, pl.ds(4 * c, 4), pl.ds(0, FIRST)]
+
     for d in (2, 3, 1):
-        start(own_piece, own_piece, (sent_x, rx.at[x]), at(xx=lax.rem(x + d, X)))
-
-    def give_core(xx):
-        piece = wb.at[rows_of(2 * xx + c)]
-        start(piece, piece, (sent_core, got_core), at(cc=1 - c))
-
-    give_core(x)
+        start(part_a(x), part_a(x), (sent_x, rxa.at[x]), at(xx=lax.rem(x + d, X)))
+    start(part_a(x), part_a(x), (sent_core, got_core), at(cc=1 - c))
 
     phase("zd_peaks")
     arrived(rp5.at[pl.ds(0, X - 1)], got_p5)
@@ -377,30 +490,60 @@
             line = jnp.where((lane_of >= lo) & (lane_of < lo + GROUP), row, line)
         peak_lanes[j : j + 1, :] = line
 
-    phase("ze_waitgx")
-    for d in (1, 3, 2):
+    phase("ze_waitlast")
+
+    def from_y(d):
+        yy = lax.rem(y + d, Y)
+        arrived(part_b(yy), ryb.at[yy])
+        start(part_b(yy), part_b(yy), (sent_core, got_core), at(cc=1 - c))
+
+    def from_x(d):
         xx = lax.rem(x + d, X)
-        arrived(wb.at[rows_of(2 * xx + c)], rx.at[xx])
-        give_core(xx)
+        arrived(part_a(xx), rxa.at[xx])
+        start(part_a(xx), part_a(xx), (sent_core, got_core), at(cc=1 - c))
+
+    from_y(1)
+    from_y(7)
+    from_y(2)
+    from_y(6)
+    from_x(1)
+    from_x(3)
+    from_y(3)
+    from_y(5)
+    from_y(4)
+    from_x(2)
 
     phase("zf_drain")
-    departed(r1.at[pl.ds(0, X * C - 1)], sent_codes)
+    departed(r1a.at[pl.ds(0, X * C - 1)], sent_1a)
+    departed(r1b.at[pl.ds(0, Y * C - 1)], sent_1b)
     departed(rp1.at[pl.ds(0, X * C - 1)], sent_pk1)
-    finish(departed, r2, sent2)
-    finish(departed, rp2, sent_p2)
-    departed(r3.at[pl.ds(0, Z - 1)], sent3)
+    either(local & first_core, departed, r2a, sent_2a, 3, 4)
+    either(local & last_core, departed, r2b, sent_2b, 3, 4)
+    either(own_c, departed, r2c, sent_2c, 1, 2)
+    either(local, departed, rp2, sent_p2, 7, 8)
+    departed(r3.at[pl.ds(0, Z - 1)], sent_3)
     departed(rp3.at[pl.ds(0, Z - 1)], sent_p3)
     departed(gz.at[pl.ds(0, Z - 1)], sent_z)
     departed(rp4.at[pl.ds(0, Y - 1)], sent_p4)
-    finish(departed, gy, sent_y)
     departed(rp5.at[pl.ds(0, X - 1)], sent_p5)
-    departed(r1.at[pl.ds(0, X - 1)], sent_x)
-    departed(r1.at[pl.ds(0, X)], sent_core)
-    arrived(r1.at[pl.ds(0, X)], got_core)
+
+    @pl.when(first_core)
+    def _():
+        either(local, departed, gya, sent_ya, 7, 8)
+
+    @pl.when(last_core)
+    def _():
+        either(local, departed, gyb, sent_yb, 7, 8)
+        either(xhalf == 0, departed, codes_b.at[0], sent_xb, 4, 3)
+
+    departed(r1b.at[pl.ds(0, Y - 1)], sent_yc)
+    departed(r1a.at[pl.ds(0, X - 1)], sent_x)
+    departed(wb.at[pl.ds(0, 2)], sent_core)
+    arrived(wb.at[pl.ds(0, 2)], got_core)
     phase(None)
 
 
-SEMS = 24
+SEMS = 34
 
 
 def store(stepped, wb, peak_lanes, out_master, out_first, out_second, weights, out_peak, sem):
@@ -419,7 +562,7 @@
     vmem = lambda *shape, dtype=f32: pltpu.VMEM(shape, dtype)
     dma = lambda n: pltpu.SemaphoreType.DMA((n,))
     own = jax.ShapeDtypeStruct((OWNED, WIDTH), f32)
-    whole = jax.ShapeDtypeStruct((ROWS, WIDTH), bf16)
+    whole = jax.ShapeDtypeStruct((X, Y, GROUP, WIDTH), bf16)
     lanes = jax.ShapeDtypeStruct((LANE_ROWS, WIDTH), f32)
     in_vmem = pl.BlockSpec(memory_space=pltpu.VMEM)
     anywhere = pl.BlockSpec(memory_space=pl.ANY)
@@ -433,15 +576,21 @@
             vmem(LANE_ROWS, WIDTH),
             vmem(ROWS, WIDTH),
             vmem(3, OWNED, WIDTH),
-            vmem(ROWS, WIDTH, dtype=bf16),
-            vmem(X * C, PIECE, WIDTH, dtype=bf16),
+            vmem(X * C, 4 * FIRST, WIDTH, dtype=bf16),
+            vmem(X, Y, LAST, WIDTH, dtype=bf16),
+            vmem(X * C, 4 * FIRST, WIDTH, dtype=bf16),
+            vmem(Y * C, 2, LAST, WIDTH, dtype=bf16),
             vmem(X * C, 4, WIDTH),
             vmem(X * C, 4, WIDTH),
-            vmem(PIECE, WIDTH),
-            vmem(8, SHARE, WIDTH),
+            vmem(4, SHARE, WIDTH),
+            vmem(4, SPLIT, WIDTH),
+            vmem(2, LAST, WIDTH),
             vmem(4, 1, WIDTH),
             vmem(Y, SHARE, WIDTH),
+            vmem(Y, SPLIT, WIDTH),
+            vmem(X, LAST, WIDTH),
             vmem(Y, 1, WIDTH),
+            vmem(SHARE, WIDTH),
             vmem(Z, OWNED, WIDTH),
             vmem(Z, OWNED, WIDTH),
             vmem(1, WIDTH),
@@ -450,14 +599,17 @@
             vmem(Z, OWNED, WIDTH),
             vmem(SHARE, WIDTH),
             vmem(SHARE, WIDTH, dtype=bf16),
+            vmem(SPLIT, WIDTH),
+            vmem(LAST, WIDTH, dtype=bf16),
             vmem(8, SHARE, WIDTH, dtype=bf16),
+            vmem(8, SPLIT, WIDTH),
             vmem(Y, 1, WIDTH),
-            vmem(PIECE, WIDTH),
+            vmem(4 * FIRST, WIDTH),
             vmem(Y, WIDTH),
             vmem(X, Y, WIDTH),
             pltpu.SemaphoreType.REGULAR,
             pltpu.SemaphoreType.REGULAR,
-            dma(X * C), dma(4), dma(SEMS), dma(X),
+            dma(X * C), dma(4), dma(SEMS), dma(X), dma(Y),
         ],
         compiler_params=pltpu.CompilerParams(
             collective_id=0, has_side_effects=True, vmem_limit_bytes=16 * 2**20
@@ -474,7 +626,7 @@
         scratch_shapes=[dma(5)],
         compiler_params=pltpu.CompilerParams(vmem_limit_bytes=8 * 2**20),
     )(*held)
-    return (updated, first, second, weights, peak.reshape(ROWS))
+    return (updated, first, second, weights.reshape(ROWS, WIDTH), peak.reshape(ROWS))
 
 
 def solution(mesh):

time: 58.3 us -> 53.8 us (0.923)
  Pallas kernels: 57.5 us -> 53 us
    pallas_call x1, Pallas kernels: 56.6 us -> 52.2 us  [body(): pl.pallas_call(kernel, out_shape=[jax.ShapeDtypeStruct((3, OWNED, WIDTH),...]
where the time goes in v3:
time: 53.8 us; the launch traced here: 53.7 us
  Pallas kernels  53 us (99%)
  between operations  0.64 us (1%)
    pallas_call x1, Pallas kernels, body(): pl.pallas_call(kernel, out_shape=[jax.ShapeDtypeStruct((3, OWNED, WIDTH),...  52.2 us

profile of v3, /device:TPU:1, one launch (start us, length us, event | category | flops | bytes accessed | tf_op | source)
XLA Modules:
  0.0 53.7 jit_solution(3352410096642240643)
XLA Ops:
  0.6 52.2 %shard_map.92 = (f32[3,3,128]{2,1,0:T(4,128)S(1)}, bf16[4,8,72,128]{3,2,1,0:T(8,128)(2,1)S(1)}, f32[18,128]{1,0:T(8,128)S(1)}) custom-call(f32[2304,128]{1,0:T(8,128)} %bitcast.4, f32[18,128]{1,0:T(8,128)} %bitcast.5, f32[3,128]{1,0:T(4,128)} %master.1, f32[3,128]{1,0:T(4,128)} %moment1.1, f32[3,128]{1,0:T(4,128)} %moment2.1), custom_call_target="tpu_custom_call" | custom-call | tf_op jit(solution)/shard_map/pallas_call | solution.py:569
  52.8 0.9 %shard_map.93 = (f32[3,128]{1,0:T(4,128)}, f32[3,128]{1,0:T(4,128)}, f32[3,128]{1,0:T(4,128)}, bf16[4,8,72,128]{3,2,1,0:T(8,128)(2,1)}, f32[18,128]{1,0:T(8,128)}) custom-call(f32[3,3,128]{2,1,0:T(4,128)S(1)} %get-tuple-element.13.stepped, bf16[4,8,72,128]{3,2,1,0:T(8,128)(2,1)S(1)} %get-tuple-element.14.wb, f32[18,128]{1,0:T(8,128)S(1)} %get-tuple-element.15.peak_lanes), custom_call_target="tpu_custom_call" | custom-call | tf_op jit(solution)/shard_map/pallas_call | solution.py:621
